TPU v7x, 16 devices: a whole 2x2x2 slice. The times are simulated.
16 devices in a mesh: ey: 2 (over z), ex: 8 (over y, x, core).
Axes of the slice: x: 2, y: 2, z: 2, core: 2. Of those that a mesh axis runs over, the one named last changes fastest.
Arguments:
- x: bfloat16 [256, 2048], P(('ey', 'ex'))
- kv_k: bfloat16 [256, 256, 16, 128], P(('ey', 'ex'))
- kv_v: bfloat16 [256, 256, 16, 128], P(('ey', 'ex'))
- lens: int32 [256], P(('ey', 'ex'))
- topk_idx: int32 [256, 8], P(('ey', 'ex'))
- gates: float32 [256, 8], P(('ey', 'ex'))
- ln1: bfloat16 [2048], replicated
- ln2: bfloat16 [2048], replicated
- wq: bfloat16 [2048, 2048], replicated
- wo: bfloat16 [2048, 2048], replicated
- ws1: bfloat16 [2048, 1024], replicated
- ws3: bfloat16 [2048, 1024], replicated
- ws2: bfloat16 [1024, 2048], replicated
- w1: bfloat16 [64, 2048, 1024], P(('ey', 'ex'))
- w3: bfloat16 [64, 2048, 1024], P(('ey', 'ex'))
- w2: bfloat16 [64, 1024, 2048], P(('ey', 'ex'))
Outputs:
- output: bfloat16 [256, 2048], P(('ey', 'ex'))
All inputs are finite; a program needn't handle non-finite values.
Results may differ from a plain program's by a relative error of at most 0.0120205.
Values are sent between devices in bfloat16 or wider.
A program may use at most 1 GiB of HBM per device.

v0:
```python
import jax
import jax.numpy as jnp
from jax import lax
from jax.sharding import PartitionSpec as P

EPS = 1e-6
BF = jnp.bfloat16
F32 = jnp.float32


def _rms(v, w):
    v = v.astype(F32)
    r = lax.rsqrt(jnp.mean(v * v, axis=-1, keepdims=True) + EPS)
    return (v * r * w.astype(F32)).astype(BF)


def _ffn(u, w1, w3, w2):
    g = jnp.dot(u, w1, preferred_element_type=F32)
    v = jnp.dot(u, w3, preferred_element_type=F32)
    z = (jax.nn.silu(g) * v).astype(BF)
    return jnp.dot(z, w2, preferred_element_type=F32).astype(BF)


def _experts(xin, w1, w3, w2):
    g = jnp.einsum('erd,edf->erf', xin, w1, preferred_element_type=F32)
    v = jnp.einsum('erd,edf->erf', xin, w3, preferred_element_type=F32)
    z = (jax.nn.silu(g) * v).astype(BF)
    return jnp.einsum('erf,efd->erd', z, w2, preferred_element_type=F32).astype(BF)


def _attn(x, kk, vv, lens, ln1, wq, wo):
    b, l, kvh, dh = kk.shape
    hq = wq.shape[1] // dh
    a = _rms(x, ln1)
    q = jnp.dot(a, wq, preferred_element_type=F32).astype(BF).reshape(b, kvh, hq // kvh, dh)
    s = jnp.einsum('bkgd,blkd->bkgl', q, kk, preferred_element_type=F32) * dh ** -0.5
    valid = jnp.arange(l)[None, :] < lens[:, None]
    s = jnp.where(valid[:, None, None, :], s, -jnp.inf)
    p = jax.nn.softmax(s, axis=-1).astype(BF)
    o = jnp.einsum('bkgl,blkd->bkgd', p, vv, preferred_element_type=F32).astype(BF)
    attn = jnp.dot(o.reshape(b, hq * dh), wo, preferred_element_type=F32)
    return (x.astype(F32) + attn).astype(BF)


def _ranks(topk, n_exp):
    chosen = (topk[..., None] == jnp.arange(n_exp)).any(axis=-2).astype(jnp.int32)
    before = jnp.cumsum(chosen, axis=-2) - chosen
    return jnp.take_along_axis(before, topk, axis=-1)


def solution(mesh):
    ey, ex = mesh.shape['ey'], mesh.shape['ex']
    ndev = ey * ex
    rows = P(('ey', 'ex'))
    rep = P()

    def local(x, kv_k, kv_v, lens, topk_idx, gates, ln1, ln2, wq, wo, ws1, ws3, ws2, w1, w3, w2):
        b, d = x.shape
        k = topk_idx.shape[1]
        edev = w1.shape[0]
        n_exp = edev * ndev
        cap = max(4, (2 * b * k + n_exp - 1) // n_exp)
        nslotv = ex * edev * ey * cap
        iy = lax.axis_index('ey')

        h = _attn(x, kv_k, kv_v, lens, ln1, wq, wo)
        u = _rms(h, ln2)

        u_g = lax.all_gather(u, 'ey')
        t_g = lax.all_gather(topk_idx, 'ey')
        g_g = lax.all_gather(gates, 'ey')

        rank = _ranks(t_g, n_exp)
        mine = (t_g // (edev * ex) == iy) & (rank < cap)
        src = jnp.arange(ey, dtype=jnp.int32)[:, None, None]
        dest = ((t_g // edev) % ex) * edev + t_g % edev
        pos = jnp.where(mine, (dest * ey + src) * cap + rank, nslotv).reshape(-1)
        tok = jnp.broadcast_to(jnp.arange(ey * b, dtype=jnp.int32).reshape(ey, b, 1), t_g.shape).reshape(-1)
        slot_tok = jnp.full((nslotv,), ey * b, jnp.int32).at[pos].set(tok, mode='drop')
        slot_gate = jnp.zeros((nslotv,), F32).at[pos].set(g_g.reshape(-1), mode='drop')
        u_pad = jnp.concatenate([u_g.reshape(ey * b, d), jnp.zeros((1, d), BF)], axis=0)

        send = u_pad[slot_tok].reshape(ex, edev, ey * cap, d)
        recv = lax.all_to_all(send, 'ex', 0, 0)
        xin = recv.transpose(1, 0, 2, 3).reshape(edev, ex * ey * cap, d)
        out = _experts(xin, w1, w3, w2)
        back = out.reshape(edev, ex, ey * cap, d).transpose(1, 0, 2, 3)
        ret = lax.all_to_all(back, 'ex', 0, 0).reshape(nslotv, d)

        partial = jnp.zeros((ey * b + 1, d), F32).at[slot_tok].add(slot_gate[:, None] * ret.astype(F32))
        routed = lax.psum_scatter(partial[: ey * b].reshape(ey, b, d), 'ey', scatter_dimension=0)
        y = h.astype(F32) + _ffn(u, ws1, ws3, ws2).astype(F32) + routed
        return y.astype(BF)

    return jax.shard_map(
        local, mesh=mesh,
        in_specs=(rows, rows, rows, rows, rows, rows, rep, rep, rep, rep, rep, rep, rep, rows, rows, rows),
        out_specs=rows, check_vma=False)
```

profile of v0, /device:TPU:0, one launch (start us, length us, event | category | flops | bytes accessed | tf_op | source)
XLA Modules:
  0.0 142.8 jit_solution(15535638354677498223)
XLA Ops:
  6.5 5.6 %all-gather.3 = s32[2,16,8]{1,2,0:T(8,128)S(1)} all-gather(s32[1,16,8]{1,2,0:T(8,128)} %bitcast.69), channel_id=2, replica_groups=mesh['ey'=2,'ex'=8] {'ey'}, dimensions={0}, use_global_device_ids=true | all-gather | bytes 1536 | tf_op jit(solution)/shard_map/all_gather | solution.py:70
  12.2 0.1 fusion.45
  12.4 0.1 reshape.173
  12.5 2.4 %gather_fusion.1 = s32[256]{0:T(256)S(1)} fusion(s32[2,16,64]{2,1,0:T(8,128)S(1)} %convert_subtract_fusion, s32[256]{0:T(256)S(1)} %reshape.173), kind=kCustom, calls=%fused_computation.1 | custom fusion | bytes 5120 | tf_op jit(solution)/shard_map/jit(take_along_axis)/gather | solution.py:48
  15.0 0.1 reshape.176
  15.1 0.1 reshape.153
  15.3 0.1 reshape.183
  15.4 1.4 scatter_custom_fusion
  16.9 0.1 fusion.40
  17.0 4.6 %convolution_convert_fusion.2 = bf16[16,2048]{1,0:T(8,128)(2,1)S(1)} fusion(bf16[2048,2048]{1,0:T(8,128)(2,1)} %param.24, bf16[16,2048]{1,0:T(8,128)(2,1)S(1)} %copy-done, f32[2048]{0:T(1024)S(1)} %convert_element_type.62, f32[16]{0:T(128)S(1)} %add_rsqrt_fusion.1), kind=kOutput, calls=%fused_computation.21 | convolution fusion | flops 134381568 | bytes 8527936 | tf_op jit(solution)/shard_map/dot_general | solution.py:35
  21.6 0.1 reshape.226
  21.8 10.2 %fusion.4 = f32[16,16,1,256]{3,2,1,0:T(1,128)S(1)} fusion(bf16[16,16,128,1]{2,3,1,0:T(2,128)(2,1)S(1)} %reshape.226, bf16[16,256,16,128]{3,2,1,0:T(8,128)(2,1)} %param.17), kind=kOutput, calls=%fused_computation.9 | convolution fusion | flops 16777216 | bytes 17104896 | tf_op jit(solution)/shard_map/bkgd,blkd->bkgl/dot_general | solution.py:36
  32.0 0.2 fusion.19
  32.3 8.8 %fusion.2 = f32[16,16,1,128]{3,2,1,0:T(1,128)S(1)} fusion(bf16[16,256,16,128]{3,2,1,0:T(8,128)(2,1)} %param.18, bf16[16,16,256,1]{2,1,0,3:T(8,128)(2,1)S(1)} %fusion.19), kind=kOutput, calls=%fused_computation.7 | convolution fusion | flops 16777216 | bytes 17039360 | tf_op jit(solution)/shard_map/bkgl,blkd->bkgd/dot_general | solution.py:40
  41.1 4.7 %multiply_reduce_fusion = (f32[16]{0:T(128)S(1)}, f32[16,2048]{1,0:T(8,128)S(1)}) fusion(bf16[2048,2048]{1,0:T(8,128)(2,1)} %param.25, bf16[2,8,16,128]{3,2,1,0:T(8,128)(2,1)S(1)} %bitcast.67, bf16[16,2048]{1,0:T(8,128)(2,1)S(1)} %copy-done), kind=kOutput, calls=%fused_computation.58 | convolution fusion | flops 134414320 | bytes 8650816 | tf_op jit(solution)/shard_map/dot_general | solution.py:41
  45.8 0.1 multiply_convert_fusion
  45.9 4.9 %all-gather.2 = bf16[32,2048]{1,0:T(8,128)(2,1)S(1)} all-gather(bf16[16,2048]{1,0:T(8,128)(2,1)S(1)} %multiply_convert_fusion), channel_id=4, replica_groups=mesh['ey'=2,'ex'=8] {'ey'}, dimensions={0}, use_global_device_ids=true | all-gather | bytes 196608 | tf_op jit(solution)/shard_map/all_gather | solution.py:69
  50.9 1.4 gather_fusion
  52.2 19.3 %all_to_all.10 = bf16[8,4,8,2048]{3,2,1,0:T(8,128)(2,1)S(1)} all-to-all(bf16[8,4,8,2048]{3,2,1,0:T(8,128)(2,1)S(1)} %bitcast.64), channel_id=1, replica_groups=mesh['ey'=2,'ex'=8] {'ex'}, dimensions={0} | all-to-all | bytes 2097152 | tf_op jit(solution)/shard_map/all_to_all | solution.py:84
  71.6 8.8 %fusion.23 = f32[4,64,1024]{2,1,0:T(8,128)S(1)} fusion(bf16[4,2048,1024]{2,1,0:T(8,128)(2,1)} %param.29, bf16[8,4,8,2048]{3,2,1,0:T(8,128)(2,1)S(1)} %all_to_all.10), kind=kOutput, calls=%fused_computation.34 | convolution fusion | flops 1073741824 | bytes 18874368 | tf_op jit(solution)/shard_map/erd,edf->erf/dot_general | solution.py:25
  80.4 16.5 %fusion.6 = bf16[4,8,8,2048]{3,2,1,0:T(8,128)(2,1)S(1)} fusion(bf16[4,1024,2048]{2,1,0:T(8,128)(2,1)} %param.31, bf16[4,2048,1024]{2,1,0:T(8,128)(2,1)} %param.30, f32[4,64,1024]{2,1,0:T(8,128)S(1)} %fusion.23, bf16[8,4,8,2048]{3,2,1,0:T(8,128)(2,1)S(1)} %all_to_all.10), kind=kOutput, calls=%fused_computation.12 | convolution fusion | flops 2149580800 | bytes 36700160 | tf_op jit(solution)/shard_map/erf,efd->erd/dot_general | solution.py:28
  96.9 1.1 copy.82
  97.9 3.6 %all-to-all-start.1 = ((bf16[8,4,8,2048]{3,2,1,0:T(8,128)(2,1)}), bf16[8,4,8,2048]{3,2,1,0:T(8,128)(2,1)S(1)}, u32[]{:S(2)}, u32[]{:S(2)}) async-start(bf16[8,4,8,2048]{3,2,1,0:T(8,128)(2,1)} %bitcast.63), calls=%async_computation.1 | async-start | bytes 2097152 | tf_op jit(solution)/shard_map/all_to_all | solution.py:88
  101.6 4.3 %all-gather.4 = f32[2,16,8]{1,2,0:T(8,128)S(1)} all-gather(f32[1,16,8]{1,2,0:T(8,128)S(1)} %bitcast.70), channel_id=3, replica_groups=mesh['ey'=2,'ex'=8] {'ey'}, dimensions={0}, use_global_device_ids=true | all-gather | bytes 1536 | tf_op jit(solution)/shard_map/all_gather | solution.py:71
  106.0 0.1 reshape.191
  106.1 1.4 scatter_custom_fusion.1
  107.5 9.3 %all-to-all-done.1 = bf16[8,4,8,2048]{3,2,1,0:T(8,128)(2,1)S(1)} async-done(((bf16[8,4,8,2048]{3,2,1,0:T(8,128)(2,1)}), bf16[8,4,8,2048]{3,2,1,0:T(8,128)(2,1)S(1)}, u32[]{:S(2)}, u32[]{:S(2)}) %all-to-all-start.1) | async-done | bytes 1048608 | tf_op jit(solution)/shard_map/all_to_all | solution.py:88
  116.8 4.0 %scatter_custom_fusion.2 = f32[33,2048]{1,0:T(8,128)S(1)} fusion(s32[256]{0:T(256)S(1)} %compare_select_fusion.1, bf16[256,2048]{1,0:T(8,128)(2,1)S(1)} %bitcast.65, f32[256]{0:T(256)S(1)} %scatter_custom_fusion.1, f32[]{:T(128)} %constant.83.clone.1), kind=kCustom, calls=%fused_computation.23 | custom fusion | flops 1572864 | bytes 1319940 | tf_op jit(solution)/shard_map/scatter-add | solution.py:90
  120.8 0.7 slice.9
  121.5 2.8 %fusion.81 = f32[16,1024]{1,0:T(8,128)S(1)} fusion(bf16[16,2048]{1,0:T(8,128)(2,1)S(1)} %multiply_convert_fusion, bf16[2048,1024]{1,0:T(8,128)(2,1)} %param.26), kind=kOutput, calls=%fused_computation.116 | convolution fusion | flops 67108864 | bytes 4325376 | tf_op jit(solution)/shard_map/dot_general | solution.py:18
  124.4 6.3 %reduce-scatter.2.cloned.1.call-done = f32[1,16,2048]{2,1,0:T(8,128)} async-done(((f32[2,16,2048]{2,1,0:T(8,128)}), f32[1,16,2048]{2,1,0:T(8,128)}) %reduce-scatter.2.cloned.1.call-update) | async-done | bytes 131088 | tf_op jit(solution)/shard_map/reduce_scatter | solution.py:91
  130.7 5.3 %fusion.10 = bf16[16,2048]{1,0:T(8,128)(2,1)} fusion(f32[16,2048]{1,0:T(8,128)S(1)} %get-tuple-element.6, bf16[1024,2048]{1,0:T(8,128)(2,1)} %param.28, bf16[16,2048]{1,0:T(8,128)(2,1)S(1)} %multiply_convert_fusion, bf16[2048,1024]{1,0:T(8,128)(2,1)} %param.27, f32[1,16,2048]{2,1,0:T(8,128)} %reduce-scatter.2.cloned.1.call-done, f32[16,1024]{1,0:T(8,128)S(1)} %fusion.81), kind=kOutput, calls=%fused_computation.18 | convolution fusion | flops 134479872 | bytes 8847360 | tf_op jit(solution)/shard_map/dot_general | solution.py:21
  (31 shorter events, 0.6 us)
Async XLA Ops:
  12.5 4.3 %copy-start.1 = (bf16[2048]{0:T(1024)(128)(2,1)S(1)}, bf16[2048]{0:T(1024)(128)(2,1)}, u32[]{:S(2)}) copy-start(bf16[2048]{0:T(1024)(128)(2,1)} %param.22) | copy-start | bytes 12292
  12.5 4.3 %copy-start = (bf16[16,2048]{1,0:T(8,128)(2,1)S(1)}, bf16[16,2048]{1,0:T(8,128)(2,1)}, u32[]{:S(2)}) copy-start(bf16[16,2048]{1,0:T(8,128)(2,1)} %param.16) | copy-start | bytes 196612
  15.0 6.8 %copy-start.4 = (s32[16]{0:T(128)S(1)}, s32[16]{0:T(128)}, u32[]{:S(2)}) copy-start(s32[16]{0:T(128)} %param.19) | copy-start | bytes 196
  41.1 4.7 %copy-start.2 = (bf16[2048]{0:T(1024)(128)(2,1)S(1)}, bf16[2048]{0:T(1024)(128)(2,1)}, u32[]{:S(2)}) copy-start(bf16[2048]{0:T(1024)(128)(2,1)} %param.23) | copy-start | bytes 12292
  80.4 21.2 %copy-start.3 = (f32[16,8]{0,1:T(8,128)S(1)}, f32[16,8]{0,1:T(8,128)}, u32[]{:S(2)}) copy-start(f32[16,8]{0,1:T(8,128)} %param.21) | copy-start | bytes 1540
  97.9 18.8 %all-to-all-start.1 = ((bf16[8,4,8,2048]{3,2,1,0:T(8,128)(2,1)}), bf16[8,4,8,2048]{3,2,1,0:T(8,128)(2,1)S(1)}, u32[]{:S(2)}, u32[]{:S(2)}) async-start(bf16[8,4,8,2048]{3,2,1,0:T(8,128)(2,1)} %bitcast.63), calls=%async_computation.1 | async-start | bytes 2097152 | tf_op jit(solution)/shard_map/all_to_all | solution.py:88
  101.5 29.2 %reduce-scatter.2.cloned.1.call-start = ((), (), s32[]{:S(2)}) async-start(), calls=%async_computation.3 | async-start | bytes 393216 | tf_op jit(solution)/shard_map/reduce_scatter | solution.py:91
Sparse Core Ops, SparseCore 0:
  121.6 8.9 reduce-scatter.1
where the time goes:
time: 143 us
  matrix products  61.8 us (43%)
  blocking collectives  34.2 us (24%)
  waiting for transfers between devices  15.6 us (11%)
  between operations  13.7 us (10%)
  local copies, waits for them, and re-layouts  9.17 us (6%)
  other arithmetic  4.8 us (3%)
  starting transfers between devices  3.6 us (3%)
    all_to_all x1, blocking collectives, local(): recv = lax.all_to_all(send, 'ex', 0, 0)  19.3 us
    dot_general x1, matrix products, _experts(): jnp.einsum('erf,efd->erd', z, w2, preferred_element_type=F32).astype(BF)  16.5 us
    dot_general x1, matrix products, _attn(): jnp.einsum('bkgd,blkd->bkgl', q, kk, preferred_element_type=F32)  10.2 us
    all_to_all x1, waiting for transfers between devices, local(): ret = lax.all_to_all(back, 'ex', 0, 0).reshape(nslotv, d)  9.31 us
    dot_general x1, matrix products, _attn(): jnp.einsum('bkgl,blkd->bkgd', p, vv, preferred_element_type=F32).astype(BF)  8.81 us
    dot_general x1, matrix products, _experts(): g = jnp.einsum('erd,edf->erf', xin, w1, preferred_element_type=F32)  8.78 us
    reduce_scatter x1, waiting for transfers between devices, local(): lax.psum_scatter(partial[:ey * b].reshape(ey, b, d), 'ey', scatter_dimens...  6.3 us
    all_gather x1, blocking collectives, local(): t_g = lax.all_gather(topk_idx, 'ey')  5.61 us
  transfers between devices with their start and end apart: 2, of which 2 were waited for; matrix products, arithmetic and copies ran while one was open for 3% of the time, Pallas kernels for 0%

commit v1 on v0

v1 whole, which is shorter than its diff:
```python
import functools

import jax
import jax.numpy as jnp
from jax import lax
from jax.experimental import pallas as pl
from jax.experimental.pallas import tpu as pltpu
from jax.sharding import PartitionSpec as P

EPS = 1e-6
BF = jnp.bfloat16
F32 = jnp.float32
I32 = jnp.int32
MESH = pl.DeviceIdType.MESH
VMEM_LIMIT = 60 * 1024 * 1024

SHORT = 32


def _iota(shape, dim):
    return lax.broadcasted_iota(I32, shape, dim)


def _dot(a, b):
    return jnp.dot(a, b, preferred_element_type=F32)


def _rms(v, w):
    v = v.astype(F32)
    r = lax.rsqrt(jnp.mean(v * v, axis=-1, keepdims=True) + EPS)
    return (v * r * w.astype(F32)).astype(BF)


def _attn_kernel(lens, x, ln1, ln2, kk, vv, wq, wo, h_out, u_out,
                 kbuf, vbuf, wqb, wob, q3, o3, posd, longs,
                 wsem, ssem, lsem):
    b, heads, dh = q3.shape
    rows = kbuf.shape[1]
    short = SHORT * heads
    d = x.shape[1]
    nw = wsem.shape[1]
    cw = d // nw
    scale = dh ** -0.5

    def wcopy(i, n):
        src, dst = ((wq, wqb), (wo, wob))[i]
        return pltpu.make_async_copy(src.at[:, pl.ds(n * cw, cw)], dst.at[:, pl.ds(n * cw, cw)], wsem.at[i, n])

    def scopy(i, t):
        src, dst = ((kk, kbuf), (vv, vbuf))[i]
        return pltpu.make_async_copy(src.at[t, pl.ds(0, short)], dst.at[t, pl.ds(0, short)], ssem.at[i])

    def lcopy(i, t):
        src, dst = ((kk, kbuf), (vv, vbuf))[i]
        rest = pl.ds(short, rows - short)
        return pltpu.make_async_copy(src.at[t, rest], dst.at[t, rest], lsem.at[i, t])

    for n in range(nw):
        wcopy(0, n).start()
    for t in range(b):
        scopy(0, t).start()
        scopy(1, t).start()

    def scan(t, n):
        @pl.when(lens[t] > SHORT)
        def _():
            longs[n] = t
            lcopy(0, t).start()
            lcopy(1, t).start()
        return n + (lens[t] > SHORT).astype(I32)

    nlong = lax.fori_loop(0, b, scan, jnp.int32(0))
    for n in range(nw):
        wcopy(1, n).start()

    col = _iota((heads, rows), 1)
    posd[...] = jnp.where(col % heads == _iota((heads, rows), 0), col // heads, jnp.int32(1 << 20))

    a = _rms(x[...], ln1[...])
    for n in range(nw):
        wcopy(0, n).wait()
        q = _dot(a, wqb[:, n * cw:(n + 1) * cw]).astype(BF).astype(F32)
        for i in range(cw // dh):
            q3[:, n * (cw // dh) + i, :] = q[:, i * dh:(i + 1) * dh]

    def scores(t, m):
        qt = q3[t].astype(BF)
        s = lax.dot_general(qt, kbuf[t, :m], (((1,), (1,)), ((), ())), preferred_element_type=F32)
        s = jnp.where(posd[:, :m] < lens[t], s * scale, -jnp.inf)
        top = jnp.max(s, axis=-1, keepdims=True)
        e = jnp.exp(s - top)
        return (e / jnp.sum(e, axis=-1, keepdims=True)).astype(BF)

    def attend(ts, m):
        ps = [scores(t, m) for t in ts]
        for t, p in zip(ts, ps):
            o3[t] = _dot(p, vbuf[t, :m]).astype(BF).astype(F32)

    for t in range(b):
        scopy(0, t).wait()
        scopy(1, t).wait()
    group = 8
    for t0 in range(0, b, group):
        attend(list(range(t0, t0 + group)), short)

    def long_pair(j, carry):
        first = 2 * j
        second = jnp.minimum(first + 1, nlong - 1)
        t0, t1 = longs[first], longs[second]
        lcopy(0, t0).wait()
        lcopy(1, t0).wait()

        @pl.when(second > first)
        def _():
            lcopy(0, t1).wait()
            lcopy(1, t1).wait()
        attend([t0, t1], rows)
        return carry

    lax.fori_loop(0, (nlong + 1) // 2, long_pair, 0)

    o = jnp.concatenate([o3[:, i, :].astype(BF) for i in range(heads)], axis=1)
    for n in range(nw):
        wcopy(1, n).wait()
        sl = slice(n * cw, (n + 1) * cw)
        h_out[:, sl] = (x[:, sl].astype(F32) + _dot(o, wob[:, sl])).astype(BF)
    u_out[...] = _rms(h_out[...], ln2[...])


def _attention(x, kk, vv, lens, ln1, ln2, wq, wo):
    b, d = x.shape
    _, l, heads, dh = kk.shape
    rows = l * heads
    vm = pl.BlockSpec(memory_space=pltpu.VMEM)
    hbm = pl.BlockSpec(memory_space=pl.ANY)
    nbytes = 2 * (2 * b * rows * dh + 2 * d * d)
    return pl.pallas_call(
        _attn_kernel,
        out_shape=[jax.ShapeDtypeStruct((b, d), BF)] * 2,
        in_specs=[pl.BlockSpec(memory_space=pltpu.SMEM), vm, vm, vm, hbm, hbm, hbm, hbm],
        out_specs=[vm, vm],
        scratch_shapes=[
            pltpu.VMEM((b, rows, dh), BF),
            pltpu.VMEM((b, rows, dh), BF),
            pltpu.VMEM((d, d), BF),
            pltpu.VMEM((d, d), BF),
            pltpu.VMEM((b, heads, dh), F32),
            pltpu.VMEM((b, heads, dh), F32),
            pltpu.VMEM((heads, rows), I32),
            pltpu.SMEM((b,), I32),
            pltpu.SemaphoreType.DMA((2, 4)),
            pltpu.SemaphoreType.DMA((2,)),
            pltpu.SemaphoreType.DMA((2, b)),
        ],
        compiler_params=pltpu.CompilerParams(vmem_limit_bytes=VMEM_LIMIT),
        cost_estimate=pl.CostEstimate(flops=4 * b * d * d, bytes_accessed=nbytes, transcendentals=0),
        name='attention',
    )(lens, x, ln1.reshape(1, d), ln2.reshape(1, d),
      kk.reshape(b, rows, dh), vv.reshape(b, rows, dh), wq, wo)


def _moe_kernel(cap, h, u, topk_t, topk, gates, ws1, ws3, ws2, w1, w3, w2, y,
                wab, wcb, place, praw, perm, ug, xin, oscr, ret, gmat,
                asem, csem, psend, precv, usend, urecv, vsend, vrecv,
                rsend, rrecv, tsend, trecv):
    b, d = h.shape
    k = topk.shape[1]
    edev = w1.shape[0]
    ff = w1.shape[2]
    ndev = praw.shape[0]
    nchip = ndev // 2
    ntok = ndev * b
    slots = edev * cap
    nslot = ndev * slots
    erow = ndev * cap
    ey, ex = lax.axis_index('ey'), lax.axis_index('ex')
    nex = nchip
    iy = lax.div(ex, 4)
    ix = lax.div(ex, 2) - 2 * iy
    core = lax.rem(ex, 2)
    me = ey * nex + ex
    chip_me = lax.div(me, 2)

    flip = lambda i, by: 1 - i if by else i
    peers = {}
    for dist in range(nchip):
        pz, py, px = flip(ey, dist // 4), flip(iy, dist // 2 % 2), flip(ix, dist % 2)
        for oc in range(2):
            pex = py * 4 + px * 2 + flip(core, oc)
            peers[dist, oc] = ((pz, pex), pz * nex + pex)
    chips = [lax.div(peers[dist, 0][1], 2) for dist in range(nchip)]

    def peer(dist, other_core):
        return peers[dist, other_core]

    def acopy(e, i):
        return pltpu.make_async_copy((w1, w3)[i].at[e], wab.at[2 * e + i], asem.at[e, i])

    def ccopy(e):
        return pltpu.make_async_copy(w2.at[e], wcb.at[e], csem.at[e])

    def shared_copies():
        return [pltpu.make_async_copy(ws1, wab.at[0], asem.at[edev, 0]),
                pltpu.make_async_copy(ws3, wab.at[1], asem.at[edev, 1]),
                pltpu.make_async_copy(ws2, wcb.at[0], csem.at[edev])]

    for e in range(edev):
        acopy(e, 0).start()
        acopy(e, 1).start()
        ccopy(e).start()

    barrier = pltpu.get_barrier_semaphore()
    for dist in range(nchip):
        for oc in range(2):
            if dist or oc:
                pl.semaphore_signal(barrier, inc=1, device_id=peer(dist, oc)[0], device_id_type=MESH)

    row, colm = _iota((nslot, ntok), 0), _iota((nslot, ntok), 1)
    row_e = lax.div(row, cap)
    row_r = (row - row_e * cap).astype(F32)
    hit = jnp.zeros((nslot, ntok), F32)
    for j in range(k):
        hit = jnp.where(row_e == topk_t[j:j + 1, :], 1.0, hit)
    ra, ca = _iota((ntok, ntok), 0), _iota((ntok, ntok), 1)
    cb = lax.div(ca, b)
    earlier = jnp.where((lax.div(ra, b) == cb) & (ra < ca), 1.0, 0.0).astype(BF)
    before = _dot(hit.astype(BF), earlier)
    mine = jnp.where((before == row_r) & (lax.div(colm, b) == me), hit, 0.0)
    place[...] = mine.astype(BF).reshape(ndev, slots, ntok)

    nret = ndev * edev * 2 * cap
    lane = _iota((b, nret), 1)
    glob = lax.div(lane, 2 * cap)
    half = lax.div(lane, cap)
    lane_r = (lane - half * cap).astype(F32)
    got = jnp.zeros((b, nret), F32)
    gate = jnp.zeros((b, nret), F32)
    for j in range(k):
        same = glob == topk[:, j:j + 1]
        got = jnp.where(same, 1.0, got)
        gate = jnp.where(same, gates[:, j:j + 1], gate)
    lower = jnp.where(_iota((b, b), 1) < _iota((b, b), 0), 1.0, 0.0).astype(BF)
    prior = _dot(lower, got.astype(BF))
    keep = (prior == lane_r) & (half - 2 * glob == core)
    gate = jnp.where(keep, gate, 0.0)
    g1 = gate.astype(BF)
    rest = gate - g1.astype(F32)
    g2 = rest.astype(BF)
    g3 = (rest - g2.astype(F32)).astype(BF)
    gmat[0:b] = g1
    gmat[b:2 * b] = g2
    gmat[2 * b:3 * b] = g3

    ug[me] = u[...]
    praw[me] = place[me]

    pl.semaphore_wait(barrier, ndev - 1)

    def ucopy(dist):
        return pltpu.make_async_remote_copy(
            src_ref=u, dst_ref=ug.at[me], send_sem=usend.at[dist], recv_sem=urecv.at[dist],
            device_id=peer(dist, 0)[0], device_id_type=MESH)

    def vcopy(dist):
        src = peer(dist, 0)[1]
        return pltpu.make_async_remote_copy(
            src_ref=u if dist == 0 else ug.at[src], dst_ref=ug.at[src],
            send_sem=vsend.at[dist], recv_sem=vrecv.at[dist],
            device_id=peer(0, 1)[0], device_id_type=MESH)

    def pcopy(dist, oc):
        to, idx = peer(dist, oc)
        return pltpu.make_async_remote_copy(
            src_ref=place.at[idx], dst_ref=praw.at[me],
            send_sem=psend.at[2 * dist + oc], recv_sem=precv.at[2 * dist + oc],
            device_id=to, device_id_type=MESH)

    others = [(dist, oc) for dist in range(nchip) for oc in range(2) if dist or oc]
    order = [7, 6, 5, 3, 4, 2, 1]
    for dist in order:
        ucopy(dist).start()
    vcopy(0).start()
    for dist, oc in others:
        pcopy(dist, oc).start()
    for dist, oc in others:
        pcopy(dist, oc).wait_recv()

    rp, cp = _iota((nslot, nslot), 0), _iota((nslot, nslot), 1)
    rsrc, rexp = lax.div(rp, cap), lax.div(rp, erow)
    want = (rsrc - rexp * ndev) * slots + rexp * cap + (rp - rsrc * cap)
    perm[...] = _dot(jnp.where(want == cp, 1.0, 0.0).astype(BF), praw[...].reshape(nslot, ntok)).astype(BF)

    for dist in [4, 2, 1, 6, 5, 3, 7]:
        ucopy(dist).wait_recv()
        vcopy(dist).start()
    for dist in range(nchip):
        vcopy(dist).wait_recv()

    nx = 4
    cx = d // nx
    for n in range(nx):
        sl = slice(n * cx, (n + 1) * cx)
        xin[:, :, sl] = _dot(perm[...], ug[:, :, sl].reshape(ntok, cx)).astype(BF).reshape(edev, erow, cx)

    def rcopy(e, dist):
        chip = chips[dist]
        return pltpu.make_async_remote_copy(
            src_ref=oscr.at[e, chip], dst_ref=ret.at[me * edev + e],
            send_sem=rsend.at[e, dist], recv_sem=rrecv.at[e, dist],
            device_id=peer(dist, 0)[0], device_id_type=MESH)

    def tcopy(e, dist):
        src = peer(dist, 0)[1]
        at = src * edev + e
        return pltpu.make_async_remote_copy(
            src_ref=oscr.at[e, chip_me] if dist == 0 else ret.at[at], dst_ref=ret.at[at],
            send_sem=tsend.at[e, dist], recv_sem=trecv.at[e, dist],
            device_id=peer(0, 1)[0], device_id_type=MESH)

    def ffn(uv, i1, i3, i2, store):
        nz = 2
        cz = ff // nz
        zs = []
        for n in range(nz):
            sl = slice(n * cz, (n + 1) * cz)
            g = _dot(uv, wab[i1, :, sl])
            v = _dot(uv, wab[i3, :, sl])
            zs.append((g / (1.0 + jnp.exp(-g)) * v).astype(BF))
        z = jnp.concatenate(zs, axis=1)
        ny = 4
        cy = d // ny
        return z, ny, cy

    def forward(e):
        for dist in [4, 2, 1, 6, 5, 3, 7]:
            rcopy(e, dist).wait_recv()
            tcopy(e, dist).start()

    for e in range(edev):
        acopy(e, 0).wait()
        acopy(e, 1).wait()
        z, ny, cy = ffn(xin[e], 2 * e, 2 * e + 1, e, None)
        ccopy(e).wait()
        for n in range(ny):
            sl = slice(n * cy, (n + 1) * cy)
            oscr[e, :, :, sl] = _dot(z, wcb[e, :, sl]).astype(BF).reshape(nchip, 2 * cap, cy)
        if e == 0:
            for c in shared_copies():
                c.start()
        for dist in order:
            rcopy(e, dist).start()
        tcopy(e, 0).start()
        ret[me * edev + e] = oscr[e, chip_me]
        if e > 0:
            forward(e - 1)

    sa, sb, sc = shared_copies()
    sa.wait()
    sb.wait()
    z, ny, cy = ffn(u[...], 0, 1, 0, None)
    sc.wait()
    shared = [_dot(z, wcb[0, :, n * cy:(n + 1) * cy]).astype(BF) for n in range(ny)]

    forward(edev - 1)
    for e in range(edev):
        for dist in range(nchip):
            tcopy(e, dist).wait_recv()
    for n in range(ny):
        sl = slice(n * cy, (n + 1) * cy)
        r = _dot(gmat[...], ret[:, :, sl].reshape(nret, cy))
        routed = r[0:b] + r[b:2 * b] + r[2 * b:3 * b]
        y[:, sl] = (h[:, sl].astype(F32) + shared[n].astype(F32) + routed).astype(BF)

    for dist, oc in others:
        pcopy(dist, oc).wait_send()
    for dist in range(1, nchip):
        ucopy(dist).wait_send()
    for dist in range(nchip):
        vcopy(dist).wait_send()
    for e in range(edev):
        for dist in range(1, nchip):
            rcopy(e, dist).wait_send()
        for dist in range(nchip):
            tcopy(e, dist).wait_send()


def _moe(h, u, topk, gates, ws1, ws3, ws2, w1, w3, w2, ndev, cap):
    b, d = h.shape
    edev, _, ff = w1.shape
    nchip = ndev // 2
    slots = edev * cap
    vm = pl.BlockSpec(memory_space=pltpu.VMEM)
    hbm = pl.BlockSpec(memory_space=pl.ANY)
    dma = pltpu.SemaphoreType.DMA
    topk_t = jnp.tile(topk.T, (1, ndev))
    return pl.pallas_call(
        functools.partial(_moe_kernel, cap),
        out_shape=jax.ShapeDtypeStruct((b, d), BF),
        in_specs=[vm] * 5 + [hbm] * 6,
        out_specs=vm,
        scratch_shapes=[
            pltpu.VMEM((2 * edev, d, ff), BF),
            pltpu.VMEM((edev, ff, d), BF),
            pltpu.VMEM((ndev, slots, ndev * b), BF),
            pltpu.VMEM((ndev, slots, ndev * b), BF),
            pltpu.VMEM((ndev * slots, ndev * b), BF),
            pltpu.VMEM((ndev, b, d), BF),
            pltpu.VMEM((edev, ndev * cap, d), BF),
            pltpu.VMEM((edev, nchip, 2 * cap, d), BF),
            pltpu.VMEM((ndev * edev, 2 * cap, d), BF),
            pltpu.VMEM((3 * b, ndev * edev * 2 * cap), BF),
            dma((edev + 1, 2)), dma((edev + 1,)),
            dma((ndev,)), dma((ndev,)),
            dma((nchip,)), dma((nchip,)), dma((nchip,)), dma((nchip,)),
            dma((edev, nchip)), dma((edev, nchip)), dma((edev, nchip)), dma((edev, nchip)),
        ],
        compiler_params=pltpu.CompilerParams(
            collective_id=0, has_side_effects=True, vmem_limit_bytes=VMEM_LIMIT),
        cost_estimate=pl.CostEstimate(
            flops=6 * (edev * ndev * cap + b) * d * ff, bytes_accessed=6 * (edev + 1) * d * ff, transcendentals=0),
        name='experts',
    )(h, u, topk_t, topk, gates, ws1, ws3, ws2, w1, w3, w2)


def solution(mesh):
    ndev = mesh.shape['ey'] * mesh.shape['ex']
    rows = P(('ey', 'ex'))
    rep = P()

    def local(x, kv_k, kv_v, lens, topk_idx, gates, ln1, ln2, wq, wo, ws1, ws3, ws2, w1, w3, w2):
        cap = 4
        h, u = _attention(x, kv_k, kv_v, lens, ln1, ln2, wq, wo)
        return _moe(h, u, topk_idx, gates, ws1, ws3, ws2, w1, w3, w2, ndev, cap)

    return jax.shard_map(
        local, mesh=mesh,
        in_specs=(rows, rows, rows, rows, rows, rows, rep, rep, rep, rep, rep, rep, rep, rows, rows, rows),
        out_specs=rows, check_vma=False)
```

time: 143 us -> 63.2 us (0.44)
  matrix products: 61.8 us -> 0 us
  Pallas kernels: 0 us -> 54.8 us
  blocking collectives: 34.2 us -> 0 us
  waiting for transfers between devices: 15.6 us -> 0 us
  between operations: 13.7 us -> 0.02 us
  other arithmetic: 4.8 us -> 0 us
  starting transfers between devices: 3.6 us -> 0 us
    dot_general x8 -> x0, matrix products: 61.8 us -> none  [the longest x1 16.5 us: _experts(): jnp.einsum('erf,efd->erd', z, w2, preferred_element_type=F32).astype(BF)]
    pallas_call x0 -> x2, Pallas kernels: none -> 54.8 us  [the longest x1 42.2 us: _moe(): pl.pallas_call(functools.partial(_moe_kernel, cap), out_shape=jax.ShapeDt...]
    all_to_all x1 -> x0, blocking collectives: 19.3 us -> none  [local(): recv = lax.all_to_all(send, 'ex', 0, 0)]
    all_gather x3 -> x0, blocking collectives: 14.9 us -> none  [the longest x1 5.61 us: local(): t_g = lax.all_gather(topk_idx, 'ey')]
    all_to_all x1 -> x0, waiting for transfers between devices: 9.31 us -> none  [local(): ret = lax.all_to_all(back, 'ex', 0, 0).reshape(nslotv, d)]
    reduce_scatter x1 -> x0, waiting for transfers between devices: 6.3 us -> none  [local(): lax.psum_scatter(partial[:ey * b].reshape(ey, b, d), 'ey', scatter_dimens...]
    unnamed x10 -> x3, local copies, waits for them, and re-layouts: 0.03 us -> 4.17 us
    scatter-add x1 -> x0, other arithmetic: 3.98 us -> none  [local(): jnp.zeros((ey * b + 1, d), F32).at[slot_tok]]
  transfers between devices with their start and end apart: 2 -> 0, of which waited for: 2 -> 0; matrix products, arithmetic and copies ran while one was open for 3% -> 0% of each run, Pallas kernels for 0% -> 0%
where the time goes in v1:
time: 63.2 us; the launch traced here: 63 us
  Pallas kernels  54.8 us (87%)
  local copies, waits for them, and re-layouts  8.12 us (13%)
    pallas_call x1, Pallas kernels, _moe(): pl.pallas_call(functools.partial(_moe_kernel, cap), out_shape=jax.ShapeDt...  42.2 us
    pallas_call x1, Pallas kernels, _attention(): pl.pallas_call(_attn_kernel, out_shape=[jax.ShapeDtypeStruct((b, d), BF)]...  12.6 us
    unnamed x3, local copies, waits for them, and re-layouts  4.17 us
    another operation x2, local copies, waits for them, and re-layouts, _moe(): topk_t = jnp.tile(topk.T, (1, ndev))  1.38 us
    reshape x1, local copies, waits for them, and re-layouts, _attention(): ln1.reshape(1, d)  1.29 us
    reshape x1, local copies, waits for them, and re-layouts, _attention(): ln2.reshape(1, d)  1.29 us

profile of v1, /device:TPU:0, one launch (start us, length us, event | category | flops | bytes accessed | tf_op | source)
XLA Modules:
  0.0 63.0 jit_solution(15361797593827162744)
XLA Ops:
  0.0 1.4 %copy.18.gates = f32[16,8]{1,0:T(8,128)} copy(f32[16,8]{0,1:T(8,128)} %param.21) | data formatting | bytes 1024 | tf_op args[5]
  1.4 1.3 %reshape.16.ln1 = bf16[1,2048]{1,0:T(2,128)(2,1)} reshape(bf16[2048]{0:T(1024)(128)(2,1)} %param.22) | data formatting | bytes 8192 | tf_op jit(solution)/shard_map/reshape | solution.py:158
  2.6 1.3 %reshape.17.ln2 = bf16[1,2048]{1,0:T(2,128)(2,1)} reshape(bf16[2048]{0:T(1024)(128)(2,1)} %param.23) | data formatting | bytes 8192 | tf_op jit(solution)/shard_map/reshape | solution.py:158
  3.9 1.3 %copy.17.topk = s32[16,8]{1,0:T(8,128)} copy(s32[16,8]{0,1:T(8,128)} %param.20) | data formatting | bytes 1024 | tf_op args[4]
  5.3 0.7 %tile.4 = s32[8,16,16]{2,1,0:T(8,128)S(1)} broadcast(s32[8,16]{1,0:T(8,128)} %bitcast.5), dimensions={0,2} | broadcast | bytes 8704 | tf_op jit(solution)/shard_map/tile | solution.py:395
  6.0 0.7 %tile.10.topk_t = s32[8,256]{1,0:T(8,128)} reshape(s32[8,16,16]{2,1,0:T(8,128)S(1)} %tile.4) | data formatting | bytes 16384 | tf_op jit(solution)/shard_map/tile | solution.py:395
  6.7 12.6 %attention.1 = (bf16[16,2048]{1,0:T(8,128)(2,1)}, bf16[16,2048]{1,0:T(8,128)(2,1)}) custom-call(s32[16]{0:T(128)} %lens.1, bf16[16,2048]{1,0:T(8,128)(2,1)} %x.1, bf16[1,2048]{1,0:T(2,128)(2,1)} %reshape.16.ln1, bf16[1,2048]{1,0:T(2,128)(2,1)} %reshape.17.ln2, bf16[16,4096,128]{2,1,0:T(8,128)(2,1)} %bitcast.3, bf16[16,4096,128]{2,1,0:T(8,128)(2,1)} %bitcast.4, ...), custom_call_target="tpu_custom_call" | custom-call | flops 268435456 | bytes 50331648 | tf_op jit(solution)/shard_map/attention/pallas_call | solution.py:137
  19.3 42.2 %experts.1 = bf16[16,2048]{1,0:T(8,128)(2,1)} custom-call(bf16[16,2048]{1,0:T(8,128)(2,1)} %get-tuple-element.7.h, bf16[16,2048]{1,0:T(8,128)(2,1)} %get-tuple-element.8.u, s32[8,256]{1,0:T(8,128)} %tile.10.topk_t, s32[16,8]{1,0:T(8,128)} %copy.17.topk, f32[16,8]{1,0:T(8,128)} %copy.18.gates, bf16[2048,1024]{1,0:T(8,128)(2,1)} %ws1.1, ...), custom_call_target="tpu_custom_call" | custom-call | flops 3422552064 | bytes 62914560 | tf_op jit(solution)/shard_map/experts/pallas_call | solution.py:396
  61.5 1.5 %copy.20 = bf16[16,2048]{1,0:T(8,128)(2,1)} copy(bf16[16,2048]{1,0:T(8,128)(2,1)} %experts.1) | data formatting | bytes 131072

commit v2 on v1

--- a/solution.py
+++ b/solution.py
@@ -28,7 +28,10 @@
 def _rms(v, w):
     v = v.astype(F32)
     r = lax.rsqrt(jnp.mean(v * v, axis=-1, keepdims=True) + EPS)
-    return (v * r * w.astype(F32)).astype(BF)
+    w = w.astype(F32)
+    n = w.shape[1]
+    parts = [(v[:, i * n:(i + 1) * n] * r * w[i:i + 1, :]).astype(BF) for i in range(w.shape[0])]
+    return jnp.concatenate(parts, axis=1)
 
 
 def _attn_kernel(lens, x, ln1, ln2, kk, vv, wq, wo, h_out, u_out,
@@ -155,19 +158,19 @@
         compiler_params=pltpu.CompilerParams(vmem_limit_bytes=VMEM_LIMIT),
         cost_estimate=pl.CostEstimate(flops=4 * b * d * d, bytes_accessed=nbytes, transcendentals=0),
         name='attention',
-    )(lens, x, ln1.reshape(1, d), ln2.reshape(1, d),
+    )(lens, x, ln1.reshape(d // 128, 128), ln2.reshape(d // 128, 128),
       kk.reshape(b, rows, dh), vv.reshape(b, rows, dh), wq, wo)
 
 
-def _moe_kernel(cap, h, u, topk_t, topk, gates, ws1, ws3, ws2, w1, w3, w2, y,
-                wab, wcb, place, praw, perm, ug, xin, oscr, ret, gmat,
-                asem, csem, psend, precv, usend, urecv, vsend, vrecv,
+def _moe_kernel(cap, h, u, topk_t, gates_t, ws1, ws3, ws2, w1, w3, w2, y,
+                wab, wcb, tmine, tall, perm, ug, xin, oscr, ret, gmat,
+                asem, csem, psend, precv, qsend, qrecv, usend, urecv, vsend, vrecv,
                 rsend, rrecv, tsend, trecv):
     b, d = h.shape
-    k = topk.shape[1]
+    k = topk_t.shape[0]
     edev = w1.shape[0]
     ff = w1.shape[2]
-    ndev = praw.shape[0]
+    ndev = ug.shape[0]
     nchip = ndev // 2
     ntok = ndev * b
     slots = edev * cap
@@ -215,18 +218,14 @@
             if dist or oc:
                 pl.semaphore_signal(barrier, inc=1, device_id=peer(dist, oc)[0], device_id_type=MESH)
 
-    row, colm = _iota((nslot, ntok), 0), _iota((nslot, ntok), 1)
-    row_e = lax.div(row, cap)
-    row_r = (row - row_e * cap).astype(F32)
-    hit = jnp.zeros((nslot, ntok), F32)
-    for j in range(k):
-        hit = jnp.where(row_e == topk_t[j:j + 1, :], 1.0, hit)
-    ra, ca = _iota((ntok, ntok), 0), _iota((ntok, ntok), 1)
-    cb = lax.div(ca, b)
-    earlier = jnp.where((lax.div(ra, b) == cb) & (ra < ca), 1.0, 0.0).astype(BF)
-    before = _dot(hit.astype(BF), earlier)
-    mine = jnp.where((before == row_r) & (lax.div(colm, b) == me), hit, 0.0)
-    place[...] = mine.astype(BF).reshape(ndev, slots, ntok)
+    lanes = tmine.shape[1]
+    tk = topk_t[...].astype(F32)
+    rep_r, rep_c = _iota((b, lanes), 0), _iota((b, lanes), 1)
+    block = me - lax.div(me, lanes // b) * (lanes // b)
+    spread = jnp.where(rep_c - block * b == rep_r, 1.0, 0.0).astype(BF)
+    tmine[...] = _dot(tk.astype(BF), spread)
+    tall[me] = tmine[...]
+    ug[me] = u[...]
 
     nret = ndev * edev * 2 * cap
     lane = _iota((b, nret), 1)
@@ -235,10 +234,13 @@
     lane_r = (lane - half * cap).astype(F32)
     got = jnp.zeros((b, nret), F32)
     gate = jnp.zeros((b, nret), F32)
+    diag = _iota((b, b), 0) == _iota((b, b), 1)
     for j in range(k):
-        same = glob == topk[:, j:j + 1]
+        pick = jnp.sum(jnp.where(diag, tk[j:j + 1, :], 0.0), axis=1, keepdims=True).astype(I32)
+        gj = jnp.sum(jnp.where(diag, gates_t[j:j + 1, :], 0.0), axis=1, keepdims=True)
+        same = glob == pick
         got = jnp.where(same, 1.0, got)
-        gate = jnp.where(same, gates[:, j:j + 1], gate)
+        gate = jnp.where(same, gj, gate)
     lower = jnp.where(_iota((b, b), 1) < _iota((b, b), 0), 1.0, 0.0).astype(BF)
     prior = _dot(lower, got.astype(BF))
     keep = (prior == lane_r) & (half - 2 * glob == core)
@@ -251,54 +253,71 @@
     gmat[b:2 * b] = g2
     gmat[2 * b:3 * b] = g3
 
-    ug[me] = u[...]
-    praw[me] = place[me]
-
-    pl.semaphore_wait(barrier, ndev - 1)
+    with jax.named_scope('barrier'):
+        pl.semaphore_wait(barrier, ndev - 1)
+
+    def across(src_ref, dst_ref, send, recv, dist, oc):
+        return pltpu.make_async_remote_copy(
+            src_ref=src_ref, dst_ref=dst_ref, send_sem=send, recv_sem=recv,
+            device_id=peer(dist, oc)[0], device_id_type=MESH)
+
+    def pcopy(dist):
+        return across(tmine, tall.at[me], psend.at[dist], precv.at[dist], dist, 0)
+
+    def qcopy(dist):
+        src = peer(dist, 0)[1]
+        return across(tmine if dist == 0 else tall.at[src], tall.at[src], qsend.at[dist], qrecv.at[dist], 0, 1)
 
     def ucopy(dist):
-        return pltpu.make_async_remote_copy(
-            src_ref=u, dst_ref=ug.at[me], send_sem=usend.at[dist], recv_sem=urecv.at[dist],
-            device_id=peer(dist, 0)[0], device_id_type=MESH)
+        return across(u, ug.at[me], usend.at[dist], urecv.at[dist], dist, 0)
 
     def vcopy(dist):
         src = peer(dist, 0)[1]
-        return pltpu.make_async_remote_copy(
-            src_ref=u if dist == 0 else ug.at[src], dst_ref=ug.at[src],
-            send_sem=vsend.at[dist], recv_sem=vrecv.at[dist],
-            device_id=peer(0, 1)[0], device_id_type=MESH)
-
-    def pcopy(dist, oc):
-        to, idx = peer(dist, oc)
-        return pltpu.make_async_remote_copy(
-            src_ref=place.at[idx], dst_ref=praw.at[me],
-            send_sem=psend.at[2 * dist + oc], recv_sem=precv.at[2 * dist + oc],
-            device_id=to, device_id_type=MESH)
-
-    others = [(dist, oc) for dist in range(nchip) for oc in range(2) if dist or oc]
+        return across(u if dist == 0 else ug.at[src], ug.at[src], vsend.at[dist], vrecv.at[dist], 0, 1)
+
     order = [7, 6, 5, 3, 4, 2, 1]
+    arrive = [4, 2, 1, 6, 5, 3, 7]
+    for dist in order:
+        pcopy(dist).start()
+    qcopy(0).start()
     for dist in order:
         ucopy(dist).start()
     vcopy(0).start()
-    for dist, oc in others:
-        pcopy(dist, oc).start()
-    for dist, oc in others:
-        pcopy(dist, oc).wait_recv()
-
-    rp, cp = _iota((nslot, nslot), 0), _iota((nslot, nslot), 1)
-    rsrc, rexp = lax.div(rp, cap), lax.div(rp, erow)
-    want = (rsrc - rexp * ndev) * slots + rexp * cap + (rp - rsrc * cap)
-    perm[...] = _dot(jnp.where(want == cp, 1.0, 0.0).astype(BF), praw[...].reshape(nslot, ntok)).astype(BF)
-
-    for dist in [4, 2, 1, 6, 5, 3, 7]:
-        ucopy(dist).wait_recv()
-        vcopy(dist).start()
-    for dist in range(nchip):
-        vcopy(dist).wait_recv()
+    with jax.named_scope('choices'):
+        for dist in arrive:
+            pcopy(dist).wait_recv()
+            qcopy(dist).start()
+        for dist in range(nchip):
+            qcopy(dist).wait_recv()
+
+    with jax.named_scope('slots'):
+        nh = lanes // b
+        tok_e = jnp.concatenate(
+            [functools.reduce(jnp.add, [tall[i * nh + n] for n in range(nh)]) for i in range(ndev // nh)], axis=1)
+        row, colm = _iota((nslot, ntok), 0), _iota((nslot, ntok), 1)
+        rsrc, rexp = lax.div(row, cap), lax.div(row, erow)
+        want = (me * edev + rexp).astype(F32)
+        hit = jnp.zeros((nslot, ntok), F32)
+        for j in range(k):
+            hit = jnp.where(want == tok_e[j:j + 1, :], 1.0, hit)
+        ra, ca = _iota((ntok, ntok), 0), _iota((ntok, ntok), 1)
+        earlier = jnp.where((lax.div(ra, b) == lax.div(ca, b)) & (ra < ca), 1.0, 0.0).astype(BF)
+        before = _dot(hit.astype(BF), earlier)
+        keep = (before == (row - rsrc * cap).astype(F32)) & (lax.div(colm, b) == rsrc - rexp * ndev)
+        perm[...] = jnp.where(keep, hit, 0.0).astype(BF)
+
+    with jax.named_scope('rows'):
+        for dist in arrive:
+            ucopy(dist).wait_recv()
+            vcopy(dist).start()
+    with jax.named_scope('rows_core'):
+        for dist in range(nchip):
+            vcopy(dist).wait_recv()
 
     nx = 4
     cx = d // nx
-    for n in range(nx):
+    with jax.named_scope('gather'):
+      for n in range(nx):
         sl = slice(n * cx, (n + 1) * cx)
         xin[:, :, sl] = _dot(perm[...], ug[:, :, sl].reshape(ntok, cx)).astype(BF).reshape(edev, erow, cx)
 
@@ -332,18 +351,22 @@
         return z, ny, cy
 
     def forward(e):
-        for dist in [4, 2, 1, 6, 5, 3, 7]:
-            rcopy(e, dist).wait_recv()
-            tcopy(e, dist).start()
+        with jax.named_scope(f'forward#e={e}'):
+            for dist in arrive:
+                rcopy(e, dist).wait_recv()
+                tcopy(e, dist).start()
 
     for e in range(edev):
-        acopy(e, 0).wait()
-        acopy(e, 1).wait()
-        z, ny, cy = ffn(xin[e], 2 * e, 2 * e + 1, e, None)
-        ccopy(e).wait()
-        for n in range(ny):
-            sl = slice(n * cy, (n + 1) * cy)
-            oscr[e, :, :, sl] = _dot(z, wcb[e, :, sl]).astype(BF).reshape(nchip, 2 * cap, cy)
+        with jax.named_scope(f'weights#e={e}'):
+            acopy(e, 0).wait()
+            acopy(e, 1).wait()
+        with jax.named_scope(f'up#e={e}'):
+            z, ny, cy = ffn(xin[e], 2 * e, 2 * e + 1, e, None)
+            ccopy(e).wait()
+        with jax.named_scope(f'down#e={e}'):
+            for n in range(ny):
+                sl = slice(n * cy, (n + 1) * cy)
+                oscr[e, :, :, sl] = _dot(z, wcb[e, :, sl]).astype(BF).reshape(nchip, 2 * cap, cy)
         if e == 0:
             for c in shared_copies():
                 c.start()
@@ -354,28 +377,31 @@
         if e > 0:
             forward(e - 1)
 
-    sa, sb, sc = shared_copies()
-    sa.wait()
-    sb.wait()
-    z, ny, cy = ffn(u[...], 0, 1, 0, None)
-    sc.wait()
-    shared = [_dot(z, wcb[0, :, n * cy:(n + 1) * cy]).astype(BF) for n in range(ny)]
+    with jax.named_scope('shared'):
+        sa, sb, sc = shared_copies()
+        sa.wait()
+        sb.wait()
+        z, ny, cy = ffn(u[...], 0, 1, 0, None)
+        sc.wait()
+        shared = [_dot(z, wcb[0, :, n * cy:(n + 1) * cy]).astype(BF) for n in range(ny)]
 
     forward(edev - 1)
-    for e in range(edev):
-        for dist in range(nchip):
-            tcopy(e, dist).wait_recv()
-    for n in range(ny):
-        sl = slice(n * cy, (n + 1) * cy)
-        r = _dot(gmat[...], ret[:, :, sl].reshape(nret, cy))
-        routed = r[0:b] + r[b:2 * b] + r[2 * b:3 * b]
-        y[:, sl] = (h[:, sl].astype(F32) + shared[n].astype(F32) + routed).astype(BF)
-
-    for dist, oc in others:
-        pcopy(dist, oc).wait_send()
+    with jax.named_scope('back_core'):
+        for e in range(edev):
+            for dist in range(nchip):
+                tcopy(e, dist).wait_recv()
+    with jax.named_scope('combine'):
+        for n in range(ny):
+            sl = slice(n * cy, (n + 1) * cy)
+            r = _dot(gmat[...], ret[:, :, sl].reshape(nret, cy))
+            routed = r[0:b] + r[b:2 * b] + r[2 * b:3 * b]
+            y[:, sl] = (h[:, sl].astype(F32) + shared[n].astype(F32) + routed).astype(BF)
+
     for dist in range(1, nchip):
+        pcopy(dist).wait_send()
         ucopy(dist).wait_send()
     for dist in range(nchip):
+        qcopy(dist).wait_send()
         vcopy(dist).wait_send()
     for e in range(edev):
         for dist in range(1, nchip):
@@ -392,17 +418,16 @@
     vm = pl.BlockSpec(memory_space=pltpu.VMEM)
     hbm = pl.BlockSpec(memory_space=pl.ANY)
     dma = pltpu.SemaphoreType.DMA
-    topk_t = jnp.tile(topk.T, (1, ndev))
     return pl.pallas_call(
         functools.partial(_moe_kernel, cap),
         out_shape=jax.ShapeDtypeStruct((b, d), BF),
-        in_specs=[vm] * 5 + [hbm] * 6,
+        in_specs=[vm] * 4 + [hbm] * 6,
         out_specs=vm,
         scratch_shapes=[
             pltpu.VMEM((2 * edev, d, ff), BF),
             pltpu.VMEM((edev, ff, d), BF),
-            pltpu.VMEM((ndev, slots, ndev * b), BF),
-            pltpu.VMEM((ndev, slots, ndev * b), BF),
+            pltpu.VMEM((topk.shape[1], 128), F32),
+            pltpu.VMEM((ndev, topk.shape[1], 128), F32),
             pltpu.VMEM((ndev * slots, ndev * b), BF),
             pltpu.VMEM((ndev, b, d), BF),
             pltpu.VMEM((edev, ndev * cap, d), BF),
@@ -410,7 +435,7 @@
             pltpu.VMEM((ndev * edev, 2 * cap, d), BF),
             pltpu.VMEM((3 * b, ndev * edev * 2 * cap), BF),
             dma((edev + 1, 2)), dma((edev + 1,)),
-            dma((ndev,)), dma((ndev,)),
+            dma((nchip,)), dma((nchip,)), dma((nchip,)), dma((nchip,)),
             dma((nchip,)), dma((nchip,)), dma((nchip,)), dma((nchip,)),
             dma((edev, nchip)), dma((edev, nchip)), dma((edev, nchip)), dma((edev, nchip)),
         ],
@@ -419,7 +444,7 @@
         cost_estimate=pl.CostEstimate(
             flops=6 * (edev * ndev * cap + b) * d * ff, bytes_accessed=6 * (edev + 1) * d * ff, transcendentals=0),
         name='experts',
-    )(h, u, topk_t, topk, gates, ws1, ws3, ws2, w1, w3, w2)
+    )(h, u, topk.T, gates.T, ws1, ws3, ws2, w1, w3, w2)
 
 
 def solution(mesh):

time: 63.2 us -> 53.9 us (0.85)
  local copies, waits for them, and re-layouts: 8.12 us -> 1.47 us
  Pallas kernels: 54.8 us -> 52.2 us
    pallas_call x1, Pallas kernels: 42.2 us -> 38.4 us  [_moe(): pl.pallas_call(functools.partial(_moe_kernel, cap), out_shape=jax.ShapeDt...]
    unnamed x3 -> x1, local copies, waits for them, and re-layouts: 4.17 us -> 1.47 us
    reshape x2 -> x0, local copies, waits for them, and re-layouts: 2.58 us -> none  [the longest x1 1.29 us: _attention(): ln1.reshape(1, d)]
    another operation x2 -> x0, local copies, waits for them, and re-layouts: 1.38 us -> none  [_moe(): topk_t = jnp.tile(topk.T, (1, ndev))]
    pallas_call x1, Pallas kernels: 12.6 us -> 13.7 us  [_attention(): pl.pallas_call(_attn_kernel, out_shape=[jax.ShapeDtypeStruct((b, d), BF)]...]
where the time goes in v2:
time: 53.9 us; the launch traced here: 53.7 us
  Pallas kernels  52.2 us (97%)
  local copies, waits for them, and re-layouts  1.47 us (3%)
    pallas_call x1, Pallas kernels, _moe(): pl.pallas_call(functools.partial(_moe_kernel, cap), out_shape=jax.ShapeDt...  38.4 us
    pallas_call x1, Pallas kernels, _attention(): pl.pallas_call(_attn_kernel, out_shape=[jax.ShapeDtypeStruct((b, d), BF)]...  13.7 us
    unnamed x1, local copies, waits for them, and re-layouts  1.47 us

profile of v2, /device:TPU:0, one launch (start us, length us, event | category | flops | bytes accessed | tf_op | source)
XLA Modules:
  0.0 53.7 jit_solution(16461244535475423902)
XLA Ops:
  0.0 13.7 %attention.1 = (bf16[16,2048]{1,0:T(8,128)(2,1)}, bf16[16,2048]{1,0:T(8,128)(2,1)}) custom-call(s32[16]{0:T(128)} %lens.1, bf16[16,2048]{1,0:T(8,128)(2,1)} %x.1, bf16[16,128]{1,0:T(8,128)(2,1)} %bitcast.8, bf16[16,128]{1,0:T(8,128)(2,1)} %bitcast.9, bf16[16,4096,128]{2,1,0:T(8,128)(2,1)} %bitcast.6, bf16[16,4096,128]{2,1,0:T(8,128)(2,1)} %bitcast.7, ...), custom_call_target="tpu_custom_call" | custom-call | flops 268435456 | bytes 50331648 | tf_op jit(solution)/shard_map/attention/pallas_call | solution.py:140
  13.7 38.4 %experts.1 = bf16[16,2048]{1,0:T(8,128)(2,1)} custom-call(bf16[16,2048]{1,0:T(8,128)(2,1)} %get-tuple-element.7.h, bf16[16,2048]{1,0:T(8,128)(2,1)} %get-tuple-element.8.u, s32[8,16]{1,0:T(8,128)} %bitcast.10, f32[8,16]{1,0:T(8,128)} %bitcast.11, bf16[2048,1024]{1,0:T(8,128)(2,1)} %ws1.1, bf16[2048,1024]{1,0:T(8,128)(2,1)} %ws3.1, bf16[1024,2048]{1,0:T(8,128)(2,1)} %ws2.1, ...), custom_call_target="tpu_custom_call" | custom-call | flops 3422552064 | bytes 62914560 | tf_op jit(solution)/shard_map/experts/pallas_call | solution.py:421
  52.2 1.5 %copy.18 = bf16[16,2048]{1,0:T(8,128)(2,1)} copy(bf16[16,2048]{1,0:T(8,128)(2,1)} %experts.1) | data formatting | bytes 131072

commit v3 on v2

v3 whole, which is shorter than its diff:
```python
import functools

import jax
import jax.numpy as jnp
from jax import lax
from jax.experimental import pallas as pl
from jax.experimental.pallas import tpu as pltpu
from jax.sharding import PartitionSpec as P

EPS = 1e-6
BF = jnp.bfloat16
F32 = jnp.float32
I32 = jnp.int32
MESH = pl.DeviceIdType.MESH
VMEM_LIMIT = 60 * 1024 * 1024

SHORT = 32


def _iota(shape, dim):
    return lax.broadcasted_iota(I32, shape, dim)


def _dot(a, b):
    return jnp.dot(a, b, preferred_element_type=F32)


def _rms(v, w):
    v = v.astype(F32)
    r = lax.rsqrt(jnp.mean(v * v, axis=-1, keepdims=True) + EPS)
    w = w.astype(F32)
    n = w.shape[1]
    parts = [(v[:, i * n:(i + 1) * n] * r * w[i:i + 1, :]).astype(BF) for i in range(w.shape[0])]
    return jnp.concatenate(parts, axis=1)


def _attn_kernel(lens, x_in, ln1_in, ln2_in, kk, vv, wq, wo, h_out, u_out,
                 kbuf, vbuf, wqb, wob, x, ln1, ln2, q3, o3, posd, longs,
                 isem, wsem, osem, ssem, lsem):
    b, heads, dh = q3.shape
    rows = kbuf.shape[1]
    short = SHORT * heads
    d = x.shape[1]
    nw = wsem.shape[0]
    cw = d // nw
    scale = dh ** -0.5

    def wcopy(n):
        return pltpu.make_async_copy(wq.at[:, pl.ds(n * cw, cw)], wqb.at[:, pl.ds(n * cw, cw)], wsem.at[n])

    def scopy(i, t):
        src, dst = ((kk, kbuf), (vv, vbuf))[i]
        return pltpu.make_async_copy(src.at[t, pl.ds(0, short)], dst.at[t, pl.ds(0, short)], ssem)

    def lcopy(i, t):
        src, dst = ((kk, kbuf), (vv, vbuf))[i]
        rest = pl.ds(short, rows - short)
        return pltpu.make_async_copy(src.at[t, rest], dst.at[t, rest], lsem.at[t])

    small = [pltpu.make_async_copy(s, t, isem) for s, t in ((x_in, x), (ln1_in, ln1), (ln2_in, ln2))]
    out_w = pltpu.make_async_copy(wo, wob, osem)
    for c in small:
        c.start()
    for n in range(nw):
        wcopy(n).start()
    for t in range(b):
        scopy(0, t).start()
        scopy(1, t).start()

    def scan(t, n):
        @pl.when(lens[t] > SHORT)
        def _():
            longs[n] = t
            lcopy(0, t).start()
            lcopy(1, t).start()
        return n + (lens[t] > SHORT).astype(I32)

    nlong = lax.fori_loop(0, b, scan, jnp.int32(0))
    out_w.start()

    pr, pc = _iota(posd.shape, 0), _iota(posd.shape, 1)
    pos = lax.div(pc, heads)
    posd[...] = jnp.where(pc - pos * heads == lax.rem(pr, heads), pos, jnp.int32(1 << 20))
    upper = _iota((2 * heads, 1), 0) >= heads

    for c in small:
        c.wait()
    a = _rms(x[...], ln1[...])
    for n in range(nw):
        with jax.named_scope(f'wait_wq#n={n}'):
            wcopy(n).wait()
        q = _dot(a, wqb[:, n * cw:(n + 1) * cw]).astype(BF).astype(F32)
        for i in range(cw // dh):
            q3[:, n * (cw // dh) + i, :] = q[:, i * dh:(i + 1) * dh]

    def both(f, v):
        m = f(v[:heads], v[heads:])
        return jnp.concatenate([m, m], axis=0)

    def scores(t, m):
        hm = m // 2
        qt = q3[t].astype(BF)
        none = jnp.zeros_like(qt)
        qq = jnp.concatenate([jnp.concatenate([qt, none], axis=1), jnp.concatenate([none, qt], axis=1)], axis=0)
        kc = jnp.concatenate([kbuf[t, :hm], kbuf[t, hm:m]], axis=1)
        s = lax.dot_general(qq, kc, (((1,), (1,)), ((), ())), preferred_element_type=F32)
        bound = jnp.where(upper, lens[t] - hm // heads, lens[t])
        s = jnp.where(posd[:, :hm] < bound, s * scale, -jnp.inf)
        top = both(jnp.maximum, jnp.max(s, axis=-1, keepdims=True))
        e = jnp.exp(s - top)
        return (e / both(jnp.add, jnp.sum(e, axis=-1, keepdims=True))).astype(BF)

    def attend(ts, m):
        hm = m // 2
        ps = [scores(t, m) for t in ts]
        for t, p in zip(ts, ps):
            vc = jnp.concatenate([vbuf[t, :hm], vbuf[t, hm:m]], axis=1)
            r = _dot(p, vc)
            o3[t] = (r[:heads, :dh] + r[heads:, dh:]).astype(BF).astype(F32)

    with jax.named_scope('wait_short'):
        for t in range(b):
            scopy(0, t).wait()
            scopy(1, t).wait()
    group = 8
    with jax.named_scope('short'):
        for t0 in range(0, b, group):
            attend(list(range(t0, t0 + group)), short)

    def long_pair(j, carry):
        first = 2 * j
        second = jnp.minimum(first + 1, nlong - 1)
        t0, t1 = longs[first], longs[second]
        with jax.named_scope('wait_long'):
            lcopy(0, t0).wait()
            lcopy(1, t0).wait()

            @pl.when(second > first)
            def _():
                lcopy(0, t1).wait()
                lcopy(1, t1).wait()
        with jax.named_scope('long'):
            attend([t0, t1], rows)
        return carry

    lax.fori_loop(0, (nlong + 1) // 2, long_pair, 0)

    with jax.named_scope('wait_wo'):
        out_w.wait()
    with jax.named_scope('wo'):
        o = jnp.concatenate([o3[:, i, :].astype(BF) for i in range(heads)], axis=1)
        no = 2
        co = d // no
        for n in range(no):
            sl = slice(n * co, (n + 1) * co)
            h_out[:, sl] = (x[:, sl].astype(F32) + _dot(o, wob[:, sl])).astype(BF)
        u_out[...] = _rms(h_out[...], ln2[...])


def _attention(x, kk, vv, lens, ln1, ln2, wq, wo):
    b, d = x.shape
    _, l, heads, dh = kk.shape
    rows = l * heads
    vm = pl.BlockSpec(memory_space=pltpu.VMEM)
    hbm = pl.BlockSpec(memory_space=pl.ANY)
    nbytes = 2 * (2 * b * rows * dh + 2 * d * d)
    dma = pltpu.SemaphoreType.DMA
    return pl.pallas_call(
        _attn_kernel,
        out_shape=[jax.ShapeDtypeStruct((b, d), BF)] * 2,
        in_specs=[pl.BlockSpec(memory_space=pltpu.SMEM)] + [hbm] * 7,
        out_specs=[vm, vm],
        scratch_shapes=[
            pltpu.VMEM((b, rows, dh), BF),
            pltpu.VMEM((b, rows, dh), BF),
            pltpu.VMEM((d, d), BF),
            pltpu.VMEM((d, d), BF),
            pltpu.VMEM((b, d), BF),
            pltpu.VMEM((d // 128, 128), BF),
            pltpu.VMEM((d // 128, 128), BF),
            pltpu.VMEM((b, heads, dh), F32),
            pltpu.VMEM((b, heads, dh), F32),
            pltpu.VMEM((2 * heads, rows // 2), I32),
            pltpu.SMEM((b,), I32),
            dma, dma((4,)), dma, dma, dma((b,)),
        ],
        compiler_params=pltpu.CompilerParams(vmem_limit_bytes=VMEM_LIMIT),
        cost_estimate=pl.CostEstimate(flops=4 * b * d * d, bytes_accessed=nbytes, transcendentals=0),
        name='attention',
    )(lens, x, ln1.reshape(d // 128, 128), ln2.reshape(d // 128, 128),
      kk.reshape(b, rows, dh), vv.reshape(b, rows, dh), wq, wo)


def _moe_kernel(cap, h_in, u_in, topk_in, gates_in, ws1, ws3, ws2, w1, w3, w2, y,
                wab, wcb, h, u, topk_t, gates_t, tmine, tall, perm, ug, xin, oscr, ret, gmat, acc,
                isem, usem, asem, csem, psend, precv, qsend, qrecv, usend, urecv, vsend, vrecv,
                rsend, rrecv, tsend, trecv):
    b, d = h.shape
    k = topk_t.shape[0]
    edev = w1.shape[0]
    ff = w1.shape[2]
    ndev = ug.shape[0]
    nchip = ndev // 2
    ntok = ndev * b
    slots = edev * cap
    nslot = ndev * slots
    erow = ndev * cap
    ey, ex = lax.axis_index('ey'), lax.axis_index('ex')
    nex = nchip
    iy = lax.div(ex, 4)
    ix = lax.div(ex, 2) - 2 * iy
    core = lax.rem(ex, 2)
    me = ey * nex + ex
    chip_me = lax.div(me, 2)

    flip = lambda i, by: 1 - i if by else i
    peers = {}
    for dist in range(nchip):
        pz, py, px = flip(ey, dist // 4), flip(iy, dist // 2 % 2), flip(ix, dist % 2)
        for oc in range(2):
            pex = py * 4 + px * 2 + flip(core, oc)
            peers[dist, oc] = ((pz, pex), pz * nex + pex)
    chips = [lax.div(peers[dist, 0][1], 2) for dist in range(nchip)]

    def peer(dist, other_core):
        return peers[dist, other_core]

    def acopy(e, i):
        return pltpu.make_async_copy((w1, w3)[i].at[e], wab.at[2 * e + i], asem.at[e])

    def ccopy(e):
        return pltpu.make_async_copy(w2.at[e], wcb.at[e], csem.at[e])

    def shared_copies():
        return [pltpu.make_async_copy(ws1, wab.at[0], asem.at[edev]),
                pltpu.make_async_copy(ws3, wab.at[1], asem.at[edev]),
                pltpu.make_async_copy(ws2, wcb.at[0], csem.at[edev])]

    def drained(ref, sem):
        pltpu.make_async_copy(ref, ref, sem).wait()

    barrier = pltpu.get_barrier_semaphore()
    for dist in range(nchip):
        for oc in range(2):
            if dist or oc:
                pl.semaphore_signal(barrier, inc=1, device_id=peer(dist, oc)[0], device_id_type=MESH)

    small = [pltpu.make_async_copy(s, t, isem.at[i])
             for i, (s, t) in enumerate(((topk_in, topk_t), (gates_in, gates_t), (h_in, h)))]
    rows_in = pltpu.make_async_copy(u_in, u, usem)
    rows_in.start()
    for c in small:
        c.start()
    for e in range(edev):
        acopy(e, 0).start()
        acopy(e, 1).start()
        ccopy(e).start()
    for c in small:
        c.wait()

    lanes = tmine.shape[1]
    tk = topk_t[...].astype(F32)
    rep_r, rep_c = _iota((b, lanes), 0), _iota((b, lanes), 1)
    block = me - lax.div(me, lanes // b) * (lanes // b)
    spread = jnp.where(rep_c - block * b == rep_r, 1.0, 0.0).astype(BF)
    tmine[...] = _dot(tk.astype(BF), spread)
    tall[me] = tmine[...]

    nret = ndev * 2 * cap
    lane = _iota((b, edev * nret), 1)
    tile = lax.div(lane, 2 * cap)
    expert = lax.div(lane, nret)
    glob = (tile - expert * ndev) * edev + expert
    half = lax.div(lane, cap)
    lane_r = (lane - half * cap).astype(F32)
    got = jnp.zeros((b, edev * nret), F32)
    gate = jnp.zeros((b, edev * nret), F32)
    diag = _iota((b, b), 0) == _iota((b, b), 1)
    for j in range(k):
        pick = jnp.sum(jnp.where(diag, tk[j:j + 1, :], 0.0), axis=1, keepdims=True).astype(I32)
        gj = jnp.sum(jnp.where(diag, gates_t[j:j + 1, :], 0.0), axis=1, keepdims=True)
        same = glob == pick
        got = jnp.where(same, 1.0, got)
        gate = jnp.where(same, gj, gate)
    lower = jnp.where(_iota((b, b), 1) < _iota((b, b), 0), 1.0, 0.0).astype(BF)
    prior = _dot(lower, got.astype(BF))
    keep = (prior == lane_r) & (half - 2 * tile == core)
    gate = jnp.where(keep, gate, 0.0)
    g1 = gate.astype(BF)
    rest = gate - g1.astype(F32)
    g2 = rest.astype(BF)
    g3 = (rest - g2.astype(F32)).astype(BF)
    gmat[0:b] = g1
    gmat[b:2 * b] = g2
    gmat[2 * b:3 * b] = g3

    with jax.named_scope('barrier'):
        pl.semaphore_wait(barrier, ndev - 1)

    def across(src_ref, dst_ref, send, recv, dist, oc):
        return pltpu.make_async_remote_copy(
            src_ref=src_ref, dst_ref=dst_ref, send_sem=send, recv_sem=recv,
            device_id=peer(dist, oc)[0], device_id_type=MESH)

    def pcopy(dist):
        return across(tmine, tall.at[me], psend, precv.at[dist], dist, 0)

    def qcopy(dist):
        src = peer(dist, 0)[1]
        return across(tmine if dist == 0 else tall.at[src], tall.at[src], qsend, qrecv, 0, 1)

    via = {3: (1, 2), 6: (2, 4), 5: (4, 1)}

    def ucopy(dist):
        if dist in via:
            first, link = via[dist]
            src = peer(first, 0)[1]
            return across(ug.at[src], ug.at[src], usend, urecv.at[dist], link, 0)
        return across(u, ug.at[me], usend, urecv.at[dist], dist, 0)

    def vcopy(dist):
        src = peer(dist, 0)[1]
        return across(u if dist == 0 else ug.at[src], ug.at[src], vsend, vrecv, 0, 1)

    order = [7, 6, 5, 3, 4, 2, 1]
    arrive = [4, 2, 1, 6, 5, 3, 7]
    for dist in order:
        pcopy(dist).start()
    qcopy(0).start()
    rows_in.wait()
    for dist in [1, 2, 4, 7]:
        ucopy(dist).start()
    vcopy(0).start()
    ug[me] = u[...]
    with jax.named_scope('rows_near'):
        for dist in [3, 6, 5]:
            first = via[dist][0]
            ucopy(first).wait_recv()
            ucopy(dist).start()
            vcopy(first).start()
    with jax.named_scope('choices'):
        for dist in arrive:
            pcopy(dist).wait_recv()
            qcopy(dist).start()
        drained(tall.at[pl.ds(0, nchip)], qrecv)

    with jax.named_scope('slots'):
        nh = lanes // b
        tok_e = jnp.concatenate(
            [functools.reduce(jnp.add, [tall[i * nh + n] for n in range(nh)]) for i in range(ndev // nh)], axis=1)
        row, colm = _iota((nslot, ntok), 0), _iota((nslot, ntok), 1)
        rsrc, rexp = lax.div(row, cap), lax.div(row, erow)
        want = (me * edev + rexp).astype(F32)
        hit = jnp.zeros((nslot, ntok), F32)
        for j in range(k):
            hit = jnp.where(want == tok_e[j:j + 1, :], 1.0, hit)
        ra, ca = _iota((ntok, ntok), 0), _iota((ntok, ntok), 1)
        earlier = jnp.where((lax.div(ra, b) == lax.div(ca, b)) & (ra < ca), 1.0, 0.0).astype(BF)
        before = _dot(hit.astype(BF), earlier)
        keep = (before == (row - rsrc * cap).astype(F32)) & (lax.div(colm, b) == rsrc - rexp * ndev)
        perm[...] = jnp.where(keep, hit, 0.0).astype(BF)

    with jax.named_scope('rows'):
        for dist in [7, 3, 6, 5]:
            ucopy(dist).wait_recv()
            vcopy(dist).start()
    with jax.named_scope('rows_core'):
        drained(ug.at[pl.ds(0, nchip)], vrecv)

    nx = 4
    cx = d // nx
    with jax.named_scope('gather'):
      for n in range(nx):
        sl = slice(n * cx, (n + 1) * cx)
        xin[:, :, sl] = _dot(perm[...], ug[:, :, sl].reshape(ntok, cx)).astype(BF).reshape(edev, erow, cx)

    def rcopy(e, dist):
        return across(oscr.at[e, chips[dist]], ret.at[e, me], rsend, rrecv.at[e, dist], dist, 0)

    def tcopy(e, dist):
        src = peer(dist, 0)[1]
        return across(oscr.at[e, chip_me] if dist == 0 else ret.at[e, src], ret.at[e, src],
                      tsend, trecv.at[e], 0, 1)

    def ffn(uv, i1, i3):
        nz = 2
        cz = ff // nz
        zs = []
        for n in range(nz):
            sl = slice(n * cz, (n + 1) * cz)
            g = _dot(uv, wab[i1, :, sl])
            v = _dot(uv, wab[i3, :, sl])
            zs.append((g / (1.0 + jnp.exp(-g)) * v).astype(BF))
        return jnp.concatenate(zs, axis=1)

    def forward(e):
        with jax.named_scope(f'forward#e={e}'):
            for dist in arrive:
                rcopy(e, dist).wait_recv()
                tcopy(e, dist).start()

    ny = 4
    cy = d // ny
    for e in range(edev):
        with jax.named_scope(f'weights#e={e}'):
            drained(wab.at[pl.ds(2 * e, 2)], asem.at[e])
        with jax.named_scope(f'up#e={e}'):
            z = ffn(xin[e], 2 * e, 2 * e + 1)
            ccopy(e).wait()
        with jax.named_scope(f'down#e={e}'):
            for n in range(ny):
                sl = slice(n * cy, (n + 1) * cy)
                oscr[e, :, :, sl] = _dot(z, wcb[e, :, sl]).astype(BF).reshape(nchip, 2 * cap, cy)
        if e == 0:
            for c in shared_copies():
                c.start()
        for dist in order:
            rcopy(e, dist).start()
        tcopy(e, 0).start()
        ret[e, me] = oscr[e, chip_me]

    def add(e):
        with jax.named_scope(f'add#e={e}'):
            drained(ret.at[e, pl.ds(0, nchip)], trecv.at[e])
            for n in range(ny):
                sl = slice(n * cy, (n + 1) * cy)
                r = _dot(gmat[:, e * nret:(e + 1) * nret], ret[e, :, :, sl].reshape(nret, cy))
                r = acc[:, sl] + (r[0:b] + r[b:2 * b] + r[2 * b:3 * b])
                if e < edev - 1:
                    acc[:, sl] = r
                else:
                    y[:, sl] = r.astype(BF)

    forward(0)
    with jax.named_scope('shared'):
        drained(wab.at[pl.ds(0, 2)], asem.at[edev])
        z = ffn(u[...], 0, 1)
        shared_copies()[2].wait()
        for n in range(ny):
            sl = slice(n * cy, (n + 1) * cy)
            acc[:, sl] = h[:, sl].astype(F32) + _dot(z, wcb[0, :, sl]).astype(BF).astype(F32)
    for e in range(1, edev):
        forward(e)
        add(e - 1)
    add(edev - 1)

    with jax.named_scope('sent'):
        drained(tall.at[pl.ds(0, nchip - 1)], psend)
        drained(tall.at[pl.ds(0, nchip)], qsend)
        drained(ug.at[pl.ds(0, nchip - 1)], usend)
        drained(ug.at[pl.ds(0, nchip)], vsend)
        drained(oscr.at[:, pl.ds(0, nchip - 1)], rsend)
        drained(oscr, tsend)


def _moe(h, u, topk, gates, ws1, ws3, ws2, w1, w3, w2, ndev, cap):
    b, d = h.shape
    k = topk.shape[1]
    edev, _, ff = w1.shape
    nchip = ndev // 2
    slots = edev * cap
    vm = pl.BlockSpec(memory_space=pltpu.VMEM)
    hbm = pl.BlockSpec(memory_space=pl.ANY)
    dma = pltpu.SemaphoreType.DMA
    return pl.pallas_call(
        functools.partial(_moe_kernel, cap),
        out_shape=jax.ShapeDtypeStruct((b, d), BF),
        in_specs=[hbm] * 10,
        out_specs=vm,
        scratch_shapes=[
            pltpu.VMEM((2 * edev, d, ff), BF),
            pltpu.VMEM((edev, ff, d), BF),
            pltpu.VMEM((b, d), BF),
            pltpu.VMEM((b, d), BF),
            pltpu.VMEM((k, b), I32),
            pltpu.VMEM((k, b), F32),
            pltpu.VMEM((k, 128), F32),
            pltpu.VMEM((ndev, k, 128), F32),
            pltpu.VMEM((ndev * slots, ndev * b), BF),
            pltpu.VMEM((ndev, b, d), BF),
            pltpu.VMEM((edev, ndev * cap, d), BF),
            pltpu.VMEM((edev, nchip, 2 * cap, d), BF),
            pltpu.VMEM((edev, ndev, 2 * cap, d), BF),
            pltpu.VMEM((3 * b, edev * ndev * 2 * cap), BF),
            pltpu.VMEM((b, d), F32),
            dma((3,)), dma, dma((edev + 1,)), dma((edev + 1,)),
            dma, dma((nchip,)), dma, dma,
            dma, dma((nchip,)), dma, dma,
            dma, dma((edev, nchip)), dma, dma((edev,)),
        ],
        compiler_params=pltpu.CompilerParams(
            collective_id=0, has_side_effects=True, vmem_limit_bytes=VMEM_LIMIT),
        cost_estimate=pl.CostEstimate(
            flops=6 * (edev * ndev * cap + b) * d * ff, bytes_accessed=6 * (edev + 1) * d * ff, transcendentals=0),
        name='experts',
    )(h, u, topk.T, gates.T, ws1, ws3, ws2, w1, w3, w2)


def solution(mesh):
    ndev = mesh.shape['ey'] * mesh.shape['ex']
    rows = P(('ey', 'ex'))
    rep = P()

    def local(x, kv_k, kv_v, lens, topk_idx, gates, ln1, ln2, wq, wo, ws1, ws3, ws2, w1, w3, w2):
        cap = 4
        h, u = _attention(x, kv_k, kv_v, lens, ln1, ln2, wq, wo)
        return _moe(h, u, topk_idx, gates, ws1, ws3, ws2, w1, w3, w2, ndev, cap)

    return jax.shard_map(
        local, mesh=mesh,
        in_specs=(rows, rows, rows, rows, rows, rows, rep, rep, rep, rep, rep, rep, rep, rows, rows, rows),
        out_specs=rows, check_vma=False)
```

time: 53.9 us -> 62 us (1.15)
  Pallas kernels: 52.2 us -> 60.4 us
    pallas_call x1, Pallas kernels: 38.4 us -> 44.3 us  [_moe(): pl.pallas_call(functools.partial(_moe_kernel, cap), out_shape=jax.ShapeDt...]
    pallas_call x1, Pallas kernels: 13.7 us -> 16.1 us  [_attention(): pl.pallas_call(_attn_kernel, out_shape=[jax.ShapeDtypeStruct((b, d), BF)]...]
where the time goes in v3:
time: 62 us; the launch traced here: 61.9 us
  Pallas kernels  60.4 us (97%)
  local copies, waits for them, and re-layouts  1.47 us (2%)
    pallas_call x1, Pallas kernels, _moe(): pl.pallas_call(functools.partial(_moe_kernel, cap), out_shape=jax.ShapeDt...  44.3 us
    pallas_call x1, Pallas kernels, _attention(): pl.pallas_call(_attn_kernel, out_shape=[jax.ShapeDtypeStruct((b, d), BF)]...  16.1 us
    unnamed x1, local copies, waits for them, and re-layouts  1.47 us

profile of v3, /device:TPU:0, one launch (start us, length us, event | category | flops | bytes accessed | tf_op | source)
XLA Modules:
  0.0 61.9 jit_solution(5647857483988427470)
XLA Ops:
  0.0 16.1 %attention.1 = (bf16[16,2048]{1,0:T(8,128)(2,1)}, bf16[16,2048]{1,0:T(8,128)(2,1)}) custom-call(s32[16]{0:T(128)} %lens.1, bf16[16,2048]{1,0:T(8,128)(2,1)} %x_in.1, bf16[16,128]{1,0:T(8,128)(2,1)} %bitcast.8, bf16[16,128]{1,0:T(8,128)(2,1)} %bitcast.9, bf16[16,4096,128]{2,1,0:T(8,128)(2,1)} %bitcast.6, bf16[16,4096,128]{2,1,0:T(8,128)(2,1)} %bitcast.7, ...), custom_call_target="tpu_custom_call" | custom-call | flops 268435456 | bytes 50331648 | tf_op jit(solution)/shard_map/attention/pallas_call | solution.py:168
  16.1 44.3 %experts.1 = bf16[16,2048]{1,0:T(8,128)(2,1)} custom-call(bf16[16,2048]{1,0:T(8,128)(2,1)} %get-tuple-element.7.h_in, bf16[16,2048]{1,0:T(8,128)(2,1)} %get-tuple-element.8.u_in, s32[8,16]{1,0:T(8,128)} %bitcast.10, f32[8,16]{1,0:T(8,128)} %bitcast.11, bf16[2048,1024]{1,0:T(8,128)(2,1)} %ws1.1, bf16[2048,1024]{1,0:T(8,128)(2,1)} %ws3.1, ...), custom_call_target="tpu_custom_call" | custom-call | flops 3422552064 | bytes 62914560 | tf_op jit(solution)/shard_map/experts/pallas_call | solution.py:465
  60.5 1.5 %copy.18 = bf16[16,2048]{1,0:T(8,128)(2,1)} copy(bf16[16,2048]{1,0:T(8,128)(2,1)} %experts.1) | data formatting | bytes 131072
